TPU v7x, 128 devices: a whole 4x4x4 slice. The times are simulated.
128 devices in a mesh: zero: 32 (over z, x, core), model: 4 (over y).
Axes of the slice: x: 4, y: 4, z: 4, core: 2. Of those that a mesh axis runs over, the one named last changes fastest.
Arguments:
- train_up: bfloat16 [12288, 49152], P('zero', 'model'), may hold values from -0.109375 to 0.109375
- low_up: bfloat16 [12288, 32], P('zero'), may hold values from -0.0546875 to 0.0546875
- high_up: bfloat16 [32, 49152], P(None, 'model'), may hold values from -1 to 1
- norm_train: float32 [12288], P(('zero', 'model')), may hold values from 0.25 to 1.75
- norm_step: float32 [12288], P(('zero', 'model')), may hold values from -0.3 to 0.3
Outputs:
- serving_up: bfloat16 [12288, 49152], P(None, ('model', 'zero'))
- scale_up: float32 [49152], P(('model', 'zero'))
- serve_norm: bfloat16 [12288], replicated
All inputs are finite; a program needn't handle non-finite values. Where the computation divides by a largest or mean magnitude, that divisor is 1e-20 or more.
Results may differ from a plain program's by a relative error of at most 0.001.
Values may be sent and summed in bfloat16 or wider, within the bound.
A program may use at most 128 MiB of HBM per device.

v0:
```python
import jax
import jax.numpy as jnp
from jax import lax
from jax.sharding import Mesh
from jax.sharding import PartitionSpec as P

D_MODEL = 12288
ZERO = ("zero_0", "zero_1", "zero_2")
ZERO_MODEL = ("zero_0", "zero_1", "zero_2", "model")
MODEL_ZERO = ("model", "zero_0", "zero_1", "zero_2")


mix_rate = 0.5


def sent_to_all(value, axis):
    length = lax.axis_size(axis)
    return lax.all_to_all(
        jnp.broadcast_to(value[None], (length, *value.shape)), axis, 0, 0, tiled=True
    )


def over_copies(value, axis):
    everything = sent_to_all(value, axis)
    return jnp.sum(everything, axis=0)


def in_order(pieces, dim):
    dims = list(pieces.shape[1:])
    dims[dim] *= pieces.shape[0]
    return jnp.moveaxis(pieces, 0, dim).reshape(dims)


def all_blocks(value, axes, sequence):
    pieces = value
    for k in sequence:
        pieces = lax.all_gather(pieces, axes[k])
    done = sequence[::-1]
    back = [done.index(k) for k in range(len(axes))]
    pieces = pieces.transpose(*back, *range(len(axes), pieces.ndim))
    return pieces.reshape(-1, *value.shape)


def gathered_by_axis(value, axes, sequence, dim):
    return in_order(all_blocks(value, axes, sequence), dim)


def local(train_up, low_up, high_up, norm_train, norm_step):
    whole_up = train_up.astype(jnp.float32) + mix_rate * jnp.dot(
        low_up, high_up, preferred_element_type=jnp.float32
    )
    total_up = over_copies(jnp.sum(jnp.abs(whole_up), axis=0), ZERO)
    scale_up = total_up / D_MODEL
    narrow_up = (whole_up / scale_up).astype(jnp.bfloat16)
    serving_up = lax.all_to_all(narrow_up, ZERO, split_axis=1, concat_axis=0, tiled=True)
    place = lax.axis_index(ZERO)
    scale_up = lax.dynamic_slice_in_dim(scale_up, place * serving_up.shape[1], serving_up.shape[1])
    serve_norm = gathered_by_axis(
        (norm_train + norm_step).astype(jnp.bfloat16), ZERO_MODEL, (0, 1, 3, 2), 0
    )
    return (serving_up, scale_up, serve_norm)


def solution(mesh):
    split = Mesh(
        mesh.devices.reshape(4, 4, 2, mesh.shape["model"]), ("zero_0", "zero_1", "zero_2", "model")
    )
    placed = (P(ZERO, "model"), P(ZERO, None), P(None, "model"), P(ZERO_MODEL), P(ZERO_MODEL))
    return jax.shard_map(
        local,
        mesh=split,
        in_specs=placed,
        out_specs=(P(None, MODEL_ZERO), P(MODEL_ZERO), P()),
        check_vma=False,
    )
```

profile of v0, /device:TPU:1, one launch (start us, length us, event | category | flops | bytes accessed | tf_op | source)
XLA Modules:
  0.0 215.9 jit_solution(12039285023806615570)
XLA Ops:
  0.6 0.0 copy-start
  0.6 1.1 copy-done
  1.8 10.7 %abs_reduce_fusion = (f32[12288]{0:T(1024)S(1)}, f32[384,12288]{1,0:T(8,128)}) fusion(bf16[384,32]{0,1:T(8,128)(2,1)} %param.6, bf16[32,12288]{1,0:T(8,128)(2,1)S(1)} %copy-done, bf16[384,12288]{1,0:T(8,128)(2,1)} %param.5), kind=kOutput, calls=%fused_computation.1 | convolution fusion | flops 325570560 | bytes 29171712 | tf_op jit(solution)/shard_map/dot_general | solution.py:49
  12.4 1.4 broadcast_in_dim.2
  13.8 31.9 %all_to_all.25 = f32[32,1,12288]{2,1,0:T(1,128)S(1)} all-to-all(f32[32,1,12288]{2,1,0:T(1,128)S(1)} %broadcast_in_dim.2), channel_id=1, replica_groups=mesh['zero_0'=4,'zero_1'=4,'zero_2'=2,'model'=4] {'zero_0','zero_1','zer..., dimensions={0} | all-to-all | bytes 3145728 | tf_op jit(solution)/shard_map/all_to_all | solution.py:18
  45.7 1.0 reduce_sum.19
  46.8 11.5 %divide_convert_fusion = bf16[384,12288]{1,0:T(8,128)(2,1)} fusion(f32[384,12288]{1,0:T(8,128)} %get-tuple-element.4, f32[12288]{0:T(1024)S(1)} %broadcast_multiply_fusion), kind=kLoop, calls=%fused_computation | loop fusion | flops 9437184 | bytes 28360704 | tf_op jit(solution)/shard_map/convert_element_type | solution.py:54
  58.3 0.0 copy-start.4
  58.3 0.0 copy-start.2
  58.3 0.0 copy-start.3
  58.3 9.0 %copy.29 = bf16[48,32,8,384]{3,2,0,1:T(8,128)(2,1)} copy(bf16[48,32,8,384]{3,2,1,0:T(8,128)(2,1)} %bitcast.16) | data formatting | bytes 18874368 | tf_op jit(solution)/shard_map/all_to_all | solution.py:55
  67.3 0.0 copy-start.1
  67.3 5.1 %all-to-all-start.1 = ((bf16[384,32,384]{2,0,1:T(8,128)(2,1)}), bf16[384,32,384]{2,0,1:T(8,128)(2,1)}, u32[]{:S(2)}, u32[]{:S(2)}) async-start(bf16[384,32,384]{2,0,1:T(8,128)(2,1)} %bitcast.15), calls=%async_computation.1 | async-start | bytes 18874368 | tf_op jit(solution)/shard_map/all_to_all | solution.py:55
  72.4 0.0 copy-done.4
  72.5 0.6 dynamic-slice
  73.7 0.0 copy-done.2
  73.7 0.0 copy-done.3
  73.7 0.2 dynamic-update-slice
  74.0 107.7 %all-reduce = bf16[384]{0:T(512)(128)(2,1)S(1)} all-reduce(bf16[384]{0:T(512)(128)(2,1)S(1)} %dynamic-update-slice), channel_id=2, replica_groups=mesh['zero_0'=4,'zero_1'=4,'zero_2'=2,'model'=4] {'zero_0'}, use_global_device_ids=true, to_apply=%add | all-reduce | flops 384 | bytes 1536
  181.7 0.1 reshape.25
  181.8 6.2 %all-gather.4 = bf16[4,4,96]{2,1,0:T(4,128)(2,1)S(1)} all-gather(bf16[1,4,96]{2,1,0:T(4,128)(2,1)S(1)} %reshape.25), channel_id=3, replica_groups=mesh['zero_0'=4,'zero_1'=4,'zero_2'=2,'model'=4] {'zero_1'}, dimensions={0}, use_global_device_ids=true | all-gather | bytes 3840 | tf_op jit(solution)/shard_map/all_gather | solution.py:37
  188.0 9.6 %all-gather.2 = bf16[16,4,96]{2,1,0:T(4,128)(2,1)S(1)} all-gather(bf16[4,4,96]{2,1,0:T(4,128)(2,1)S(1)} %all-gather.4), channel_id=4, replica_groups=mesh['zero_0'=4,'zero_1'=4,'zero_2'=2,'model'=4] {'model'}, dimensions={0}, use_global_device_ids=true | all-gather | bytes 15360 | tf_op jit(solution)/shard_map/all_gather | solution.py:37
  197.6 7.6 %all-gather.3 = bf16[8,4,4,96]{3,1,0,2:T(4,128)(2,1)S(1)} all-gather(bf16[4,4,4,96]{3,1,0,2:T(4,128)(2,1)S(1)} %bitcast.19), channel_id=5, replica_groups=mesh['zero_0'=4,'zero_1'=4,'zero_2'=2,'model'=4] {'zero_2'}, dimensions={0}, use_global_device_ids=true | all-gather | bytes 36864 | tf_op jit(solution)/shard_map/all_gather | solution.py:37
  205.2 0.7 reshape_reshape.3
  205.9 0.7 dynamic_slice.3
  206.6 0.0 all-to-all-done.1
  206.6 9.3 %copy.33 = bf16[12288,384]{1,0:T(8,128)(2,1)} copy(bf16[12288,384]{1,0:T(8,128)(2,1)} %bitcast.1) | data formatting | bytes 18874368
  215.9 0.0 copy-done.1
  (5 shorter events, 0.0 us)
Async XLA Ops:
  0.6 1.1 copy-start
  58.3 14.1 %copy-start.4 = (u32[128]{0:T(128)S(1)}, u32[128]{0:T(128)}, u32[]{:S(2)}) copy-start(u32[128]{0:T(128)} %constant.35) | copy-start | bytes 1540
  58.3 15.4 %copy-start.2 = (f32[96]{0:T(128)S(1)}, f32[96]{0:T(128)}, u32[]{:S(2)}) copy-start(f32[96]{0:T(128)} %param.8) | copy-start | bytes 1156
  58.3 15.4 %copy-start.3 = (f32[96]{0:T(128)S(1)}, f32[96]{0:T(128)}, u32[]{:S(2)}) copy-start(f32[96]{0:T(128)} %param.9) | copy-start | bytes 1156
  67.3 148.5 %copy-start.1 = (bf16[32,12288]{1,0:T(8,128)(2,1)S(1)}, bf16[32,12288]{1,0:T(8,128)(2,1)}, u32[]{:S(2)}) copy-start(bf16[32,12288]{1,0:T(8,128)(2,1)} %param.7) | copy-start | bytes 2359300
  67.3 139.3 %all-to-all-start.1 = ((bf16[384,32,384]{2,0,1:T(8,128)(2,1)}), bf16[384,32,384]{2,0,1:T(8,128)(2,1)}, u32[]{:S(2)}, u32[]{:S(2)}) async-start(bf16[384,32,384]{2,0,1:T(8,128)(2,1)} %bitcast.15), calls=%async_computation.1 | async-start | bytes 18874368 | tf_op jit(solution)/shard_map/all_to_all | solution.py:55
where the time goes:
time: 217 us; the launch traced here: 216 us
  blocking collectives  163 us (75%)
  local copies, waits for them, and re-layouts  23.2 us (11%)
  other arithmetic  12.6 us (6%)
  matrix products  10.7 us (5%)
  starting transfers between devices  5.09 us (2%)
    unnamed x1, blocking collectives  108 us
    all_to_all x1, blocking collectives, sent_to_all(): lax.all_to_all(jnp.broadcast_to(value[None], (length, *value.shape)), axi...  31.9 us
    all_gather x3, blocking collectives, all_blocks(): pieces = lax.all_gather(pieces, axes[k])  23.4 us
    convert_element_type x1, other arithmetic, local(): narrow_up = (whole_up / scale_up).astype(jnp.bfloat16)  11.5 us
    unnamed x15, local copies, waits for them, and re-layouts  11.3 us
    dot_general x1, matrix products, local(): jnp.dot(low_up, high_up, preferred_element_type=jnp.float32)  10.7 us
    all_to_all x1, local copies, waits for them, and re-layouts, local(): lax.all_to_all(narrow_up, ZERO, split_axis=1, concat_axis=0, tiled=True)  9.03 us
    all_to_all x1, starting transfers between devices, local(): lax.all_to_all(narrow_up, ZERO, split_axis=1, concat_axis=0, tiled=True)  5.09 us
  transfers between devices with their start and end apart: 1, of which 0 were waited for; matrix products, arithmetic and copies ran while one was open for 1% of the time, Pallas kernels for 0%

commit v1 on v0

v1 whole, which is shorter than its diff:
```python
import jax
import jax.numpy as jnp
from jax import lax
from jax.experimental import pallas as pl
from jax.experimental.pallas import tpu as pltpu
from jax.sharding import Mesh
from jax.sharding import PartitionSpec as P

D_MODEL = 12288
ROWS = 384
COLS = 384
RANK = 32
PIECE = 96
ZERO = ("zero_0", "zero_1", "zero_2")
ZERO_MODEL = ("zero_0", "zero_1", "zero_2", "model")
MODEL_ZERO = ("model", "zero_0", "zero_1", "zero_2")
MESH = pl.DeviceIdType.MESH

mix_rate = 0.5

PHASES = (
    ((2, 2),),
    ((2, 0), (0, 2)),
    ((1, 1), (3, 3)),
    ((1, 3), (3, 1)),
    ((1, 2), (3, 0)),
    ((3, 2), (1, 0)),
    ((2, 1), (0, 3)),
    ((2, 3), (0, 1)),
)
BIG = ((0, 0, 1),) + tuple((z, x, c) for phase in PHASES for x, z in phase for c in range(2))
AHEAD = 3
CHIPS = tuple((z, x) for z in range(4) for x in range(4) if (z, x) != (0, 0))
TILE = 128
PART = 768


def exchange(
    train, low, high, norm_train, norm_step, whole, scale, norm,
    recv, high_mine, norm_mine, low_cols, low_all, norm_all, sums, norm_rows,
    big_send, big_recv, low_send, low_recv, norm_send, norm_recv, local_sem,
):
    z, x, core, y = (lax.axis_index(a) for a in ZERO_MODEL)
    chip = z * 4 + x
    me = chip * 2 + core

    def at(dz, dx, dc, dy=0):
        return (lax.rem(z + dz, 4), lax.rem(x + dx, 4), lax.rem(core + dc, 2), lax.rem(y + dy, 4))

    barrier = pltpu.get_barrier_semaphore()
    for dz, dx, dc in BIG:
        pl.semaphore_signal(barrier, inc=1, device_id=at(dz, dx, dc), device_id_type=MESH)
    for dy in (1, 2, 3):
        pl.semaphore_signal(barrier, inc=1, device_id=at(0, 0, 0, dy), device_id_type=MESH)

    own = pltpu.make_async_copy(
        train.at[:, pl.ds(pl.multiple_of(me * COLS, 128), COLS)],
        recv.at[pl.ds(pl.multiple_of(me * ROWS, ROWS), ROWS)],
        local_sem.at[0],
    )
    own.start()
    get_high = pltpu.make_async_copy(
        high.at[:, pl.ds(pl.multiple_of(me * COLS, 128), COLS)], high_mine, local_sem.at[1]
    )
    get_high.start()

    get_low = pltpu.make_async_copy(
        low.at[pl.ds(pl.multiple_of(y * 8, 8), 8)], low_all.at[core, y, chip], local_sem.at[2]
    )
    get_low.start()
    get_norm = [
        pltpu.make_async_copy(ref, norm_mine.at[i], local_sem.at[3 + i])
        for i, ref in enumerate((norm_train, norm_step))
    ]
    for copy in get_norm:
        copy.start()
    norm_all[core, y, chip] = jnp.zeros((1, 128), jnp.float32)
    sums[...] = jnp.zeros_like(sums)
    for copy in get_norm:
        copy.wait()
    norm_all[core, y, chip, :, pl.ds(0, PIECE)] = norm_mine[0] + norm_mine[1]

    pl.semaphore_wait(barrier, len(BIG) + 3)
    get_low.wait()

    def big(k):
        dz, dx, dc = BIG[k]
        there = at(dz, dx, dc)
        column = (there[0] * 8 + there[1] * 2 + there[2]) * COLS
        return pltpu.make_async_remote_copy(
            src_ref=train.at[:, pl.ds(pl.multiple_of(column, 128), COLS)],
            dst_ref=recv.at[pl.ds(pl.multiple_of(me * ROWS, ROWS), ROWS)],
            send_sem=big_send.at[k],
            recv_sem=big_recv.at[k],
            device_id=there,
            device_id_type=MESH,
        )

    def small(ref, send, got, k, there):
        return pltpu.make_async_remote_copy(
            src_ref=ref, dst_ref=ref, send_sem=send.at[k], recv_sem=got.at[k],
            device_id=there, device_id_type=MESH,
        )

    bigs = [big(k) for k in range(len(BIG))]
    for copy in bigs[:AHEAD]:
        copy.start()
    smalls = []
    for k, (dz, dx) in enumerate(CHIPS):
        there = at(dz, dx, 0)
        smalls.append(small(low_all.at[core, y, chip], low_send, low_recv, k, there))
        smalls.append(small(norm_all.at[core, y, chip], norm_send, norm_recv, k, there))
    for copy in smalls:
        copy.start()
    for copy in bigs[AHEAD:]:
        copy.start()

    for copy in smalls:
        copy.wait()
    smalls = []
    for dy in (1, 2, 3):
        there = at(0, 0, 0, dy)
        smalls.append(small(low_all.at[core, y], low_send, low_recv, 14 + dy, there))
        smalls.append(small(norm_all.at[core, y], norm_send, norm_recv, 14 + dy, there))
    for copy in smalls:
        copy.start()
    for copy in smalls:
        copy.wait()
    there = at(0, 0, 1)
    smalls = [
        small(low_all.at[core], low_send, low_recv, 18, there),
        small(norm_all.at[core], norm_send, norm_recv, 18, there),
    ]
    for copy in smalls:
        copy.start()
    for copy in smalls:
        copy.wait()

    for c in range(2):
        line = jnp.zeros((16, 384), jnp.float32)
        for q in range(4):
            part = norm_all[c, q].reshape(16, 128)
            part = jnp.concatenate([part, jnp.zeros((16, 256), jnp.float32)], axis=1)
            line = line + (pltpu.roll(part, q * PIECE, 1) if q else part)
        for j in range(3):
            norm_rows[pl.ds(3 * c + j, 16, stride=6), :] = line[:, j * 128 : j * 128 + 128]
    norm[...] = norm_rows[...].astype(jnp.bfloat16)

    own.wait()
    get_high.wait()
    right = (high_mine[...].astype(jnp.float32) * mix_rate).astype(jnp.bfloat16)

    def add(source_chip, source_core):
        low_cols[...] = jnp.concatenate(
            [low_all[source_core, q, source_chip].astype(jnp.float32) for q in range(4)], axis=0
        ).T.astype(jnp.bfloat16)
        first = (source_chip * 2 + source_core) * ROWS

        @pl.loop(0, ROWS // TILE)
        def _(i):
            start = pl.multiple_of(i * TILE, TILE)
            rows = pl.ds(pl.multiple_of(first + start, TILE), TILE)
            product = jnp.dot(
                low_cols[pl.ds(start, TILE)], right, preferred_element_type=jnp.float32
            )
            value = recv[rows].astype(jnp.float32) + product
            whole[rows] = value
            sums[...] += jnp.sum(jnp.abs(value).reshape(TILE // 8, 8, COLS), axis=0)

    add(chip, core)
    for k, (dz, dx, dc) in enumerate(BIG):
        bigs[k].wait_recv()
        from_z, from_x, from_core, _ = at(4 - dz, 4 - dx, dc)
        add(from_z * 4 + from_x, from_core)
    scale[...] = jnp.sum(sums[...], axis=0, keepdims=True) / D_MODEL
    for copy in bigs:
        copy.wait_send()


def finish(whole, scale, norm, serving, scale_out, norm_out, staged, sems):
    scale_out[...] = scale[0]
    norm_out[...] = norm[...]
    inverse = 1.0 / scale[...]
    copies = []
    for i in range(D_MODEL // PART):
        rows = pl.ds(i * PART, PART)

        @pl.loop(0, PART // 64)
        def _(j):
            inner = pl.ds(pl.multiple_of(i * PART + j * 64, 64), 64)
            staged[inner] = (whole[inner] * inverse).astype(jnp.bfloat16)

        copy = pltpu.make_async_copy(staged.at[rows], serving.at[rows], sems.at[i])
        copy.start()
        copies.append(copy)
    for copy in copies:
        copy.wait()


def local(train_up, low_up, high_up, norm_train, norm_step):
    vmem = pl.BlockSpec(memory_space=pltpu.VMEM)
    hbm = pl.BlockSpec(memory_space=pltpu.HBM)
    n = len(BIG)
    dma = pltpu.SemaphoreType.DMA
    inputs = (
        train_up, low_up.T, high_up, norm_train.reshape(1, PIECE), norm_step.reshape(1, PIECE)
    )
    whole, scale, norm = pl.pallas_call(
        exchange,
        name="exchange",
        out_shape=(
            pltpu.VMEM((D_MODEL, COLS), jnp.float32),
            jax.ShapeDtypeStruct((1, COLS), jnp.float32),
            jax.ShapeDtypeStruct((PIECE, 128), jnp.bfloat16),
        ),
        in_specs=[hbm] * 5,
        out_specs=(vmem, vmem, vmem),
        scratch_shapes=[
            pltpu.VMEM((D_MODEL, COLS), jnp.bfloat16),
            pltpu.VMEM((RANK, COLS), jnp.bfloat16),
            pltpu.VMEM((2, 1, PIECE), jnp.float32),
            pltpu.VMEM((ROWS, RANK), jnp.bfloat16),
            pltpu.VMEM((2, 4, 16, 8, ROWS), jnp.bfloat16),
            pltpu.VMEM((2, 4, 16, 1, 128), jnp.float32),
            pltpu.VMEM((8, COLS), jnp.float32),
            pltpu.VMEM((PIECE, 128), jnp.float32),
            dma((n,)), dma((n,)), dma((19,)), dma((19,)), dma((19,)), dma((19,)), dma((5,)),
        ],
        compiler_params=pltpu.CompilerParams(
            collective_id=0, has_side_effects=True, vmem_limit_bytes=16 << 20
        ),
        cost_estimate=pl.CostEstimate(flops=300_000_000, bytes_accessed=40_000_000, transcendentals=0),
    )(*[pltpu.with_memory_space_constraint(array, pltpu.HBM) for array in inputs])
    serving_up, scale_up, serve_norm = pl.pallas_call(
        finish,
        name="finish",
        out_shape=(
            jax.ShapeDtypeStruct((D_MODEL, COLS), jnp.bfloat16),
            jax.ShapeDtypeStruct((COLS,), jnp.float32),
            jax.ShapeDtypeStruct((PIECE, 128), jnp.bfloat16),
        ),
        in_specs=[vmem, vmem, vmem],
        out_specs=(hbm, vmem, vmem),
        scratch_shapes=[pltpu.VMEM((D_MODEL, COLS), jnp.bfloat16), dma((D_MODEL // PART,))],
        compiler_params=pltpu.CompilerParams(vmem_limit_bytes=12 << 20),
        cost_estimate=pl.CostEstimate(flops=10_000_000, bytes_accessed=10_000_000, transcendentals=0),
    )(pltpu.with_memory_space_constraint(whole, pltpu.VMEM), scale, norm)
    return serving_up, scale_up, serve_norm.reshape(D_MODEL)


def solution(mesh):
    split = Mesh(
        mesh.devices.reshape(4, 4, 2, mesh.shape["model"]), ("zero_0", "zero_1", "zero_2", "model")
    )
    placed = (P(ZERO, "model"), P(ZERO, None), P(None, "model"), P(ZERO_MODEL), P(ZERO_MODEL))
    return jax.shard_map(
        local,
        mesh=split,
        in_specs=placed,
        out_specs=(P(None, MODEL_ZERO), P(MODEL_ZERO), P()),
        check_vma=False,
    )
```

time: 217 us -> 122 us (0.56)
  blocking collectives: 163 us -> 0 us
  Pallas kernels: 0 us -> 121 us
  local copies, waits for them, and re-layouts: 23.2 us -> 0 us
  other arithmetic: 12.6 us -> 0 us
  matrix products: 10.7 us -> 0 us
  starting transfers between devices: 5.09 us -> 0 us
    pallas_call x0 -> x2, Pallas kernels: none -> 121 us  [the longest x1 117 us: local(): pl.pallas_call(exchange, name='exchange', out_shape=(pltpu.VMEM((D_MODEL,...]
    unnamed x1 -> x0, blocking collectives: 108 us -> none
    all_to_all x1 -> x0, blocking collectives: 31.9 us -> none  [sent_to_all(): lax.all_to_all(jnp.broadcast_to(value[None], (length, *value.shape)), axi...]
    all_gather x3 -> x0, blocking collectives: 23.4 us -> none  [all_blocks(): pieces = lax.all_gather(pieces, axes[k])]
    convert_element_type x2 -> x0, other arithmetic: 11.5 us -> none  [the longest x1 11.5 us: local(): narrow_up = (whole_up / scale_up).astype(jnp.bfloat16)]
    unnamed x15 -> x0, local copies, waits for them, and re-layouts: 11.3 us -> none
    dot_general x1 -> x0, matrix products: 10.7 us -> none  [local(): jnp.dot(low_up, high_up, preferred_element_type=jnp.float32)]
    all_to_all x1 -> x0, local copies, waits for them, and re-layouts: 9.03 us -> none  [local(): lax.all_to_all(narrow_up, ZERO, split_axis=1, concat_axis=0, tiled=True)]
  transfers between devices with their start and end apart: 1 -> 0, of which waited for: 0 -> 0; matrix products, arithmetic and copies ran while one was open for 1% -> 0% of each run, Pallas kernels for 0% -> 0%
where the time goes in v1:
time: 122 us
  Pallas kernels  121 us (99%)
    pallas_call x1, Pallas kernels, local(): pl.pallas_call(exchange, name='exchange', out_shape=(pltpu.VMEM((D_MODEL,...  117 us
    pallas_call x1, Pallas kernels, local(): pl.pallas_call(finish, name='finish', out_shape=(jax.ShapeDtypeStruct((D_...  4.5 us

profile of v1, /device:TPU:1, one launch (start us, length us, event | category | flops | bytes accessed | tf_op | source)
XLA Modules:
  0.0 121.9 jit_solution(16637497510095323049)
XLA Ops:
  0.6 116.8 %exchange.1 = (f32[12288,384]{1,0:T(8,128)S(1)}, f32[1,384]{1,0:T(1,128)S(1)}, bf16[96,128]{1,0:T(8,128)(2,1)S(1)}) custom-call(bf16[384,12288]{1,0:T(8,128)(2,1)} %train.1, bf16[32,384]{1,0:T(8,128)(2,1)} %bitcast.4, bf16[32,12288]{1,0:T(8,128)(2,1)} %high.1, f32[1,96]{1,0:T(1,128)} %bitcast.5, f32[1,96]{1,0:T(1,128)} %bitcast.6), custom_call_target="tpu_custom_call" | custom-call | flops 300000000 | bytes 40000000 | tf_op jit(solution)/shard_map/exchange/pallas_call | solution.py:208
  117.4 4.5 %finish.1 = (bf16[12288,384]{1,0:T(8,128)(2,1)}, f32[384]{0:T(512)}, bf16[96,128]{1,0:T(8,128)(2,1)}) custom-call(f32[12288,384]{1,0:T(8,128)S(1)} %get-tuple-element.9.whole, f32[1,384]{1,0:T(1,128)S(1)} %get-tuple-element.10.scale, bf16[96,128]{1,0:T(8,128)(2,1)S(1)} %get-tuple-element.11.norm), custom_call_target="tpu_custom_call" | custom-call | flops 10000000 | bytes 10000000 | tf_op jit(solution)/shard_map/finish/pallas_call | solution.py:234

commit v2 on v1

--- a/solution.py
+++ b/solution.py
@@ -19,26 +19,30 @@
 mix_rate = 0.5
 
 PHASES = (
-    ((2, 2),),
-    ((2, 0), (0, 2)),
     ((1, 1), (3, 3)),
     ((1, 3), (3, 1)),
     ((1, 2), (3, 0)),
     ((3, 2), (1, 0)),
     ((2, 1), (0, 3)),
     ((2, 3), (0, 1)),
+    ((2, 2),),
+    ((2, 0), (0, 2)),
 )
-BIG = ((0, 0, 1),) + tuple((z, x, c) for phase in PHASES for x, z in phase for c in range(2))
-AHEAD = 3
-CHIPS = tuple((z, x) for z in range(4) for x in range(4) if (z, x) != (0, 0))
+FIRST = 1
+CHIPS = tuple((z, x) for phase in PHASES for x, z in phase)
+EARLY = sum(len(phase) for phase in PHASES[:FIRST])
+NEAR = ((0, 0, 1),) + tuple(
+    (z, x, c) for z in (0, 1, 3) for x in (0, 1, 3) for c in range(2) if (z, x) != (0, 0)
+)
 TILE = 128
-PART = 768
+PARTS = (256, 512, 768) + (1536,) * 7
+BODY = 256
 
 
 def exchange(
     train, low, high, norm_train, norm_step, whole, scale, norm,
     recv, high_mine, norm_mine, low_cols, low_all, norm_all, sums, norm_rows,
-    big_send, big_recv, low_send, low_recv, norm_send, norm_recv, local_sem,
+    heard, big_send, big_recv, low_send, low_recv, norm_send, norm_recv, local_sem,
 ):
     z, x, core, y = (lax.axis_index(a) for a in ZERO_MODEL)
     chip = z * 4 + x
@@ -48,7 +52,7 @@
         return (lax.rem(z + dz, 4), lax.rem(x + dx, 4), lax.rem(core + dc, 2), lax.rem(y + dy, 4))
 
     barrier = pltpu.get_barrier_semaphore()
-    for dz, dx, dc in BIG:
+    for dz, dx, dc in NEAR:
         pl.semaphore_signal(barrier, inc=1, device_id=at(dz, dx, dc), device_id_type=MESH)
     for dy in (1, 2, 3):
         pl.semaphore_signal(barrier, inc=1, device_id=at(0, 0, 0, dy), device_id_type=MESH)
@@ -80,19 +84,14 @@
         copy.wait()
     norm_all[core, y, chip, :, pl.ds(0, PIECE)] = norm_mine[0] + norm_mine[1]
 
-    pl.semaphore_wait(barrier, len(BIG) + 3)
-    get_low.wait()
-
-    def big(k):
-        dz, dx, dc = BIG[k]
-        there = at(dz, dx, dc)
-        column = (there[0] * 8 + there[1] * 2 + there[2]) * COLS
+    def big(place, i, target):
+        column = (place[0] * 8 + place[1] * 2 + target) * COLS
         return pltpu.make_async_remote_copy(
             src_ref=train.at[:, pl.ds(pl.multiple_of(column, 128), COLS)],
             dst_ref=recv.at[pl.ds(pl.multiple_of(me * ROWS, ROWS), ROWS)],
-            send_sem=big_send.at[k],
-            recv_sem=big_recv.at[k],
-            device_id=there,
+            send_sem=big_send.at[2 * i + target],
+            recv_sem=big_recv.at[2 * i + core],
+            device_id=(place[0], place[1], target, y),
             device_id_type=MESH,
         )
 
@@ -102,9 +101,25 @@
             device_id=there, device_id_type=MESH,
         )
 
-    bigs = [big(k) for k in range(len(BIG))]
-    for copy in bigs[:AHEAD]:
-        copy.start()
+    pl.semaphore_wait(barrier, len(NEAR) + 3)
+    other = pltpu.make_async_remote_copy(
+        src_ref=train.at[:, pl.ds(pl.multiple_of((chip * 2 + 1 - core) * COLS, 128), COLS)],
+        dst_ref=recv.at[pl.ds(pl.multiple_of(me * ROWS, ROWS), ROWS)],
+        send_sem=big_send.at[30],
+        recv_sem=big_recv.at[30],
+        device_id=at(0, 0, 1),
+        device_id_type=MESH,
+    )
+    bigs = [
+        big(at(dz, dx, 0), i, target) for i, (dz, dx) in enumerate(CHIPS) for target in range(2)
+    ]
+    other.start()
+    for copy in bigs[: 2 * EARLY]:
+        copy.start()
+    for dz, dx, dc in NEAR:
+        pl.semaphore_signal(heard, inc=1, device_id=at(dz, dx, dc), device_id_type=MESH)
+    get_low.wait()
+    pl.semaphore_wait(heard, len(NEAR))
     smalls = []
     for k, (dz, dx) in enumerate(CHIPS):
         there = at(dz, dx, 0)
@@ -112,7 +127,7 @@
         smalls.append(small(norm_all.at[core, y, chip], norm_send, norm_recv, k, there))
     for copy in smalls:
         copy.start()
-    for copy in bigs[AHEAD:]:
+    for copy in bigs[2 * EARLY :]:
         copy.start()
 
     for copy in smalls:
@@ -146,53 +161,74 @@
             norm_rows[pl.ds(3 * c + j, 16, stride=6), :] = line[:, j * 128 : j * 128 + 128]
     norm[...] = norm_rows[...].astype(jnp.bfloat16)
 
-    own.wait()
     get_high.wait()
     right = (high_mine[...].astype(jnp.float32) * mix_rate).astype(jnp.bfloat16)
 
-    def add(source_chip, source_core):
+    @pl.loop(0, 32)
+    def _(source):
         low_cols[...] = jnp.concatenate(
-            [low_all[source_core, q, source_chip].astype(jnp.float32) for q in range(4)], axis=0
+            [low_all[source % 2, q, source // 2].astype(jnp.float32) for q in range(4)], axis=0
         ).T.astype(jnp.bfloat16)
-        first = (source_chip * 2 + source_core) * ROWS
 
         @pl.loop(0, ROWS // TILE)
         def _(i):
             start = pl.multiple_of(i * TILE, TILE)
-            rows = pl.ds(pl.multiple_of(first + start, TILE), TILE)
-            product = jnp.dot(
+            whole[pl.ds(pl.multiple_of(source * ROWS + start, TILE), TILE)] = jnp.dot(
                 low_cols[pl.ds(start, TILE)], right, preferred_element_type=jnp.float32
             )
-            value = recv[rows].astype(jnp.float32) + product
+
+    def add(source):
+        @pl.loop(0, ROWS // TILE)
+        def _(i):
+            rows = pl.ds(pl.multiple_of(source * ROWS + i * TILE, TILE), TILE)
+            value = recv[rows].astype(jnp.float32) + whole[rows]
             whole[rows] = value
             sums[...] += jnp.sum(jnp.abs(value).reshape(TILE // 8, 8, COLS), axis=0)
 
-    add(chip, core)
-    for k, (dz, dx, dc) in enumerate(BIG):
-        bigs[k].wait_recv()
-        from_z, from_x, from_core, _ = at(4 - dz, 4 - dx, dc)
-        add(from_z * 4 + from_x, from_core)
+    own.wait()
+    add(me)
+    other.wait()
+    add(chip * 2 + 1 - core)
+    for i, (dz, dx) in enumerate(CHIPS):
+        from_z, from_x, _, _ = at(4 - dz, 4 - dx, 0)
+        for source_core in range(2):
+            source = (from_z * 4 + from_x) * 2 + source_core
+            pltpu.make_async_remote_copy(
+                src_ref=train.at[:, pl.ds(0, COLS)],
+                dst_ref=recv.at[pl.ds(pl.multiple_of(source * ROWS, ROWS), ROWS)],
+                send_sem=big_send.at[2 * i + source_core],
+                recv_sem=big_recv.at[2 * i + source_core],
+                device_id=(from_z, from_x, source_core, y),
+                device_id_type=MESH,
+            ).wait_recv()
+            add(source)
     scale[...] = jnp.sum(sums[...], axis=0, keepdims=True) / D_MODEL
     for copy in bigs:
         copy.wait_send()
 
 
-def finish(whole, scale, norm, serving, scale_out, norm_out, staged, sems):
-    scale_out[...] = scale[0]
-    norm_out[...] = norm[...]
+def finish(whole, scale, norm, serving, scale_out, norm_out, staged, scale_line, sems, small_sems):
+    scale_line[...] = scale[0]
     inverse = 1.0 / scale[...]
-    copies = []
-    for i in range(D_MODEL // PART):
-        rows = pl.ds(i * PART, PART)
-
-        @pl.loop(0, PART // 64)
+    copies = [
+        pltpu.make_async_copy(scale_line, scale_out, small_sems.at[0]),
+        pltpu.make_async_copy(norm, norm_out, small_sems.at[1]),
+    ]
+    for copy in copies:
+        copy.start()
+    first = 0
+    for i, length in enumerate(PARTS):
+
+        @pl.loop(0, length // BODY)
         def _(j):
-            inner = pl.ds(pl.multiple_of(i * PART + j * 64, 64), 64)
+            inner = pl.ds(pl.multiple_of(first + j * BODY, BODY), BODY)
             staged[inner] = (whole[inner] * inverse).astype(jnp.bfloat16)
 
+        rows = pl.ds(first, length)
         copy = pltpu.make_async_copy(staged.at[rows], serving.at[rows], sems.at[i])
         copy.start()
         copies.append(copy)
+        first += length
     for copy in copies:
         copy.wait()
 
@@ -200,7 +236,6 @@
 def local(train_up, low_up, high_up, norm_train, norm_step):
     vmem = pl.BlockSpec(memory_space=pltpu.VMEM)
     hbm = pl.BlockSpec(memory_space=pltpu.HBM)
-    n = len(BIG)
     dma = pltpu.SemaphoreType.DMA
     inputs = (
         train_up, low_up.T, high_up, norm_train.reshape(1, PIECE), norm_step.reshape(1, PIECE)
@@ -224,7 +259,7 @@
             pltpu.VMEM((2, 4, 16, 1, 128), jnp.float32),
             pltpu.VMEM((8, COLS), jnp.float32),
             pltpu.VMEM((PIECE, 128), jnp.float32),
-            dma((n,)), dma((n,)), dma((19,)), dma((19,)), dma((19,)), dma((19,)), dma((5,)),
+            pltpu.SemaphoreType.REGULAR, dma((31,)), dma((31,)), dma((19,)), dma((19,)), dma((19,)), dma((19,)), dma((5,)),
         ],
         compiler_params=pltpu.CompilerParams(
             collective_id=0, has_side_effects=True, vmem_limit_bytes=16 << 20
@@ -240,8 +275,12 @@
             jax.ShapeDtypeStruct((PIECE, 128), jnp.bfloat16),
         ),
         in_specs=[vmem, vmem, vmem],
-        out_specs=(hbm, vmem, vmem),
-        scratch_shapes=[pltpu.VMEM((D_MODEL, COLS), jnp.bfloat16), dma((D_MODEL // PART,))],
+        out_specs=(hbm, hbm, hbm),
+        scratch_shapes=[
+            pltpu.VMEM((D_MODEL, COLS), jnp.bfloat16),
+            pltpu.VMEM((COLS,), jnp.float32),
+            dma((len(PARTS),)), dma((2,)),
+        ],
         compiler_params=pltpu.CompilerParams(vmem_limit_bytes=12 << 20),
         cost_estimate=pl.CostEstimate(flops=10_000_000, bytes_accessed=10_000_000, transcendentals=0),
     )(pltpu.with_memory_space_constraint(whole, pltpu.VMEM), scale, norm)

time: 122 us -> 120 us (0.984)
  Pallas kernels: 121 us -> 119 us
    pallas_call x1, Pallas kernels: 117 us -> 116 us  [local(): pl.pallas_call(exchange, name='exchange', out_shape=(pltpu.VMEM((D_MODEL,...]
where the time goes in v2:
time: 120 us
  Pallas kernels  119 us (99%)
    pallas_call x1, Pallas kernels, local(): pl.pallas_call(exchange, name='exchange', out_shape=(pltpu.VMEM((D_MODEL,...  116 us
    pallas_call x1, Pallas kernels, local(): pl.pallas_call(finish, name='finish', out_shape=(jax.ShapeDtypeStruct((D_...  3.77 us

profile of v2, /device:TPU:1, one launch (start us, length us, event | category | flops | bytes accessed | tf_op | source)
XLA Modules:
  0.0 119.9 jit_solution(2353345577128676072)
XLA Ops:
  0.6 115.5 %exchange.1 = (f32[12288,384]{1,0:T(8,128)S(1)}, f32[1,384]{1,0:T(1,128)S(1)}, bf16[96,128]{1,0:T(8,128)(2,1)S(1)}) custom-call(bf16[384,12288]{1,0:T(8,128)(2,1)} %train.1, bf16[32,384]{1,0:T(8,128)(2,1)} %bitcast.4, bf16[32,12288]{1,0:T(8,128)(2,1)} %high.1, f32[1,96]{1,0:T(1,128)} %bitcast.5, f32[1,96]{1,0:T(1,128)} %bitcast.6), custom_call_target="tpu_custom_call" | custom-call | flops 300000000 | bytes 40000000 | tf_op jit(solution)/shard_map/exchange/pallas_call | solution.py:243
  116.2 3.8 %finish.1 = (bf16[12288,384]{1,0:T(8,128)(2,1)}, f32[384]{0:T(512)}, bf16[96,128]{1,0:T(8,128)(2,1)}) custom-call(f32[12288,384]{1,0:T(8,128)S(1)} %get-tuple-element.9.whole, f32[1,384]{1,0:T(1,128)S(1)} %get-tuple-element.10.scale, bf16[96,128]{1,0:T(8,128)(2,1)S(1)} %get-tuple-element.11.norm), custom_call_target="tpu_custom_call" | custom-call | flops 10000000 | bytes 10000000 | tf_op jit(solution)/shard_map/finish/pallas_call | solution.py:269

commit v3 on v2

--- a/solution.py
+++ b/solution.py
@@ -19,16 +19,17 @@
 mix_rate = 0.5
 
 PHASES = (
+    ((1, 3), (3, 1)),
     ((1, 1), (3, 3)),
-    ((1, 3), (3, 1)),
+    ((3, 2), (1, 0)),
     ((1, 2), (3, 0)),
-    ((3, 2), (1, 0)),
+    ((2, 3), (0, 1)),
     ((2, 1), (0, 3)),
-    ((2, 3), (0, 1)),
     ((2, 2),),
     ((2, 0), (0, 2)),
 )
 FIRST = 1
+MORE = 4
 CHIPS = tuple((z, x) for phase in PHASES for x, z in phase)
 EARLY = sum(len(phase) for phase in PHASES[:FIRST])
 NEAR = ((0, 0, 1),) + tuple(
@@ -47,6 +48,8 @@
     z, x, core, y = (lax.axis_index(a) for a in ZERO_MODEL)
     chip = z * 4 + x
     me = chip * 2 + core
+    slot = chip * (1 - core) + (x * 4 + z) * core
+    line = pl.ds((z * (1 - core) + x * core) * 4, 4)
 
     def at(dz, dx, dc, dy=0):
         return (lax.rem(z + dz, 4), lax.rem(x + dx, 4), lax.rem(core + dc, 2), lax.rem(y + dy, 4))
@@ -69,7 +72,7 @@
     get_high.start()
 
     get_low = pltpu.make_async_copy(
-        low.at[pl.ds(pl.multiple_of(y * 8, 8), 8)], low_all.at[core, y, chip], local_sem.at[2]
+        low.at[pl.ds(pl.multiple_of(y * 8, 8), 8)], low_all.at[core, y, slot], local_sem.at[2]
     )
     get_low.start()
     get_norm = [
@@ -78,11 +81,11 @@
     ]
     for copy in get_norm:
         copy.start()
-    norm_all[core, y, chip] = jnp.zeros((1, 128), jnp.float32)
+    norm_all[core, y, slot] = jnp.zeros((1, 128), jnp.float32)
     sums[...] = jnp.zeros_like(sums)
     for copy in get_norm:
         copy.wait()
-    norm_all[core, y, chip, :, pl.ds(0, PIECE)] = norm_mine[0] + norm_mine[1]
+    norm_all[core, y, slot, :, pl.ds(0, PIECE)] = norm_mine[0] + norm_mine[1]
 
     def big(place, i, target):
         column = (place[0] * 8 + place[1] * 2 + target) * COLS
@@ -120,45 +123,49 @@
         pl.semaphore_signal(heard, inc=1, device_id=at(dz, dx, dc), device_id_type=MESH)
     get_low.wait()
     pl.semaphore_wait(heard, len(NEAR))
-    smalls = []
-    for k, (dz, dx) in enumerate(CHIPS):
-        there = at(dz, dx, 0)
-        smalls.append(small(low_all.at[core, y, chip], low_send, low_recv, k, there))
-        smalls.append(small(norm_all.at[core, y, chip], norm_send, norm_recv, k, there))
+    stages = (
+        (at(core * d, (1 - core) * d, 0), slot) for d in (1, 2, 3)
+    ), (
+        (at((1 - core) * d, core * d, 0), line) for d in (1, 2, 3)
+    ), (
+        (at(0, 0, 0, d), pl.ds(0, 16)) for d in (1, 2, 3)
+    )
+    started = 2 * EARLY
+    for n, (stage, until) in enumerate(zip(stages, (started + MORE, len(bigs), len(bigs)))):
+        smalls = []
+        for k, (there, part) in enumerate(stage):
+            smalls.append(small(low_all.at[core, y, part], low_send, low_recv, 3 * n + k, there))
+            smalls.append(small(norm_all.at[core, y, part], norm_send, norm_recv, 3 * n + k, there))
+        for copy in smalls:
+            copy.start()
+        for copy in bigs[started:until]:
+            copy.start()
+        started = until
+        for copy in smalls:
+            copy.wait()
+    there = at(0, 0, 1)
+    smalls = [
+        small(low_all.at[core], low_send, low_recv, 9, there),
+        small(norm_all.at[core], norm_send, norm_recv, 9, there),
+    ]
     for copy in smalls:
         copy.start()
-    for copy in bigs[2 * EARLY :]:
-        copy.start()
-
     for copy in smalls:
         copy.wait()
-    smalls = []
-    for dy in (1, 2, 3):
-        there = at(0, 0, 0, dy)
-        smalls.append(small(low_all.at[core, y], low_send, low_recv, 14 + dy, there))
-        smalls.append(small(norm_all.at[core, y], norm_send, norm_recv, 14 + dy, there))
-    for copy in smalls:
-        copy.start()
-    for copy in smalls:
-        copy.wait()
-    there = at(0, 0, 1)
-    smalls = [
-        small(low_all.at[core], low_send, low_recv, 18, there),
-        small(norm_all.at[core], norm_send, norm_recv, 18, there),
-    ]
-    for copy in smalls:
-        copy.start()
-    for copy in smalls:
-        copy.wait()
 
     for c in range(2):
-        line = jnp.zeros((16, 384), jnp.float32)
+        row = jnp.zeros((16, 384), jnp.float32)
         for q in range(4):
             part = norm_all[c, q].reshape(16, 128)
             part = jnp.concatenate([part, jnp.zeros((16, 256), jnp.float32)], axis=1)
-            line = line + (pltpu.roll(part, q * PIECE, 1) if q else part)
+            row = row + (pltpu.roll(part, q * PIECE, 1) if q else part)
         for j in range(3):
-            norm_rows[pl.ds(3 * c + j, 16, stride=6), :] = line[:, j * 128 : j * 128 + 128]
+            lanes = row[:, j * 128 : j * 128 + 128]
+            if c == 0:
+                norm_rows[pl.ds(j, 16, stride=6), :] = lanes
+            else:
+                for i in range(4):
+                    norm_rows[pl.ds(6 * i + 3 + j, 4, stride=24), :] = lanes[4 * i : 4 * i + 4]
     norm[...] = norm_rows[...].astype(jnp.bfloat16)
 
     get_high.wait()
@@ -166,8 +173,11 @@
 
     @pl.loop(0, 32)
     def _(source):
+        source_core, source_chip = source % 2, source // 2
+        crossed = (source_chip % 4) * 4 + source_chip // 4
+        place = source_chip * (1 - source_core) + crossed * source_core
         low_cols[...] = jnp.concatenate(
-            [low_all[source % 2, q, source // 2].astype(jnp.float32) for q in range(4)], axis=0
+            [low_all[source_core, q, place].astype(jnp.float32) for q in range(4)], axis=0
         ).T.astype(jnp.bfloat16)
 
         @pl.loop(0, ROWS // TILE)
@@ -259,7 +269,7 @@
             pltpu.VMEM((2, 4, 16, 1, 128), jnp.float32),
             pltpu.VMEM((8, COLS), jnp.float32),
             pltpu.VMEM((PIECE, 128), jnp.float32),
-            pltpu.SemaphoreType.REGULAR, dma((31,)), dma((31,)), dma((19,)), dma((19,)), dma((19,)), dma((19,)), dma((5,)),
+            pltpu.SemaphoreType.REGULAR, dma((31,)), dma((31,)), dma((10,)), dma((10,)), dma((10,)), dma((10,)), dma((5,)),
         ],
         compiler_params=pltpu.CompilerParams(
             collective_id=0, has_side_effects=True, vmem_limit_bytes=16 << 20

time: 120 us -> 119 us (level)
  no operation moved by 1% of the time
where the time goes in v3:
time: 119 us
  Pallas kernels  118 us (99%)
    pallas_call x1, Pallas kernels, local(): pl.pallas_call(exchange, name='exchange', out_shape=(pltpu.VMEM((D_MODEL,...  114 us
    pallas_call x1, Pallas kernels, local(): pl.pallas_call(finish, name='finish', out_shape=(jax.ShapeDtypeStruct((D_...  3.77 us

profile of v3, /device:TPU:1, one launch (start us, length us, event | category | flops | bytes accessed | tf_op | source)
XLA Modules:
  0.0 118.9 jit_solution(1777019645892333906)
XLA Ops:
  0.6 114.5 %exchange.1 = (f32[12288,384]{1,0:T(8,128)S(1)}, f32[1,384]{1,0:T(1,128)S(1)}, bf16[96,128]{1,0:T(8,128)(2,1)S(1)}) custom-call(bf16[384,12288]{1,0:T(8,128)(2,1)} %train.1, bf16[32,384]{1,0:T(8,128)(2,1)} %bitcast.4, bf16[32,12288]{1,0:T(8,128)(2,1)} %high.1, f32[1,96]{1,0:T(1,128)} %bitcast.5, f32[1,96]{1,0:T(1,128)} %bitcast.6), custom_call_target="tpu_custom_call" | custom-call | flops 300000000 | bytes 40000000 | tf_op jit(solution)/shard_map/exchange/pallas_call | solution.py:253
  115.1 3.8 %finish.1 = (bf16[12288,384]{1,0:T(8,128)(2,1)}, f32[384]{0:T(512)}, bf16[96,128]{1,0:T(8,128)(2,1)}) custom-call(f32[12288,384]{1,0:T(8,128)S(1)} %get-tuple-element.9.whole, f32[1,384]{1,0:T(1,128)S(1)} %get-tuple-element.10.scale, bf16[96,128]{1,0:T(8,128)(2,1)S(1)} %get-tuple-element.11.norm), custom_call_target="tpu_custom_call" | custom-call | flops 10000000 | bytes 10000000 | tf_op jit(solution)/shard_map/finish/pallas_call | solution.py:279

commit v4 on v3

--- a/solution.py
+++ b/solution.py
@@ -25,10 +25,10 @@
     ((1, 2), (3, 0)),
     ((2, 3), (0, 1)),
     ((2, 1), (0, 3)),
-    ((2, 2),),
-    ((2, 0), (0, 2)),
+    ((0, 2),),
+    ((2, 2), (2, 0)),
 )
-FIRST = 1
+FIRST = 2
 MORE = 4
 CHIPS = tuple((z, x) for phase in PHASES for x, z in phase)
 EARLY = sum(len(phase) for phase in PHASES[:FIRST])
@@ -114,8 +114,13 @@
         device_id_type=MESH,
     )
     bigs = [
-        big(at(dz, dx, 0), i, target) for i, (dz, dx) in enumerate(CHIPS) for target in range(2)
+        big(at(dz, dx, 0), i, target)
+        for i, (dz, dx) in enumerate(CHIPS[:-2])
+        for target in range(2)
     ]
+    across = jnp.minimum(z, 1)
+    for turn in (across, 1 - across):
+        bigs += [big(at(2 * turn, 2, 0), len(CHIPS) - 1 - turn, target) for target in range(2)]
     other.start()
     for copy in bigs[: 2 * EARLY]:
         copy.start()

time: 119 us -> 119 us (level)
  no operation moved by 1% of the time
where the time goes in v4:
time: 119 us
  Pallas kernels  118 us (99%)
    pallas_call x1, Pallas kernels, local(): pl.pallas_call(exchange, name='exchange', out_shape=(pltpu.VMEM((D_MODEL,...  114 us
    pallas_call x1, Pallas kernels, local(): pl.pallas_call(finish, name='finish', out_shape=(jax.ShapeDtypeStruct((D_...  3.77 us

profile of v4, /device:TPU:1, one launch (start us, length us, event | category | flops | bytes accessed | tf_op | source)
XLA Modules:
  0.0 118.9 jit_solution(17902216554261315214)
XLA Ops:
  0.6 114.5 %exchange.1 = (f32[12288,384]{1,0:T(8,128)S(1)}, f32[1,384]{1,0:T(1,128)S(1)}, bf16[96,128]{1,0:T(8,128)(2,1)S(1)}) custom-call(bf16[384,12288]{1,0:T(8,128)(2,1)} %train.1, bf16[32,384]{1,0:T(8,128)(2,1)} %bitcast.4, bf16[32,12288]{1,0:T(8,128)(2,1)} %high.1, f32[1,96]{1,0:T(1,128)} %bitcast.5, f32[1,96]{1,0:T(1,128)} %bitcast.6), custom_call_target="tpu_custom_call" | custom-call | flops 300000000 | bytes 40000000 | tf_op jit(solution)/shard_map/exchange/pallas_call | solution.py:258
  115.1 3.8 %finish.1 = (bf16[12288,384]{1,0:T(8,128)(2,1)}, f32[384]{0:T(512)}, bf16[96,128]{1,0:T(8,128)(2,1)}) custom-call(f32[12288,384]{1,0:T(8,128)S(1)} %get-tuple-element.9.whole, f32[1,384]{1,0:T(1,128)S(1)} %get-tuple-element.10.scale, bf16[96,128]{1,0:T(8,128)(2,1)S(1)} %get-tuple-element.11.norm), custom_call_target="tpu_custom_call" | custom-call | flops 10000000 | bytes 10000000 | tf_op jit(solution)/shard_map/finish/pallas_call | solution.py:284

commit v5 on v3

--- a/solution.py
+++ b/solution.py
@@ -28,8 +28,8 @@
     ((2, 2),),
     ((2, 0), (0, 2)),
 )
-FIRST = 1
-MORE = 4
+FIRST = 2
+MORE = 8
 CHIPS = tuple((z, x) for phase in PHASES for x, z in phase)
 EARLY = sum(len(phase) for phase in PHASES[:FIRST])
 NEAR = ((0, 0, 1),) + tuple(

time: 119 us -> 119 us (level)
  no operation moved by 1% of the time
where the time goes in v5:
time: 119 us
  Pallas kernels  118 us (99%)
    pallas_call x1, Pallas kernels, local(): pl.pallas_call(exchange, name='exchange', out_shape=(pltpu.VMEM((D_MODEL,...  115 us
    pallas_call x1, Pallas kernels, local(): pl.pallas_call(finish, name='finish', out_shape=(jax.ShapeDtypeStruct((D_...  3.77 us

profile of v5, /device:TPU:1, one launch (start us, length us, event | category | flops | bytes accessed | tf_op | source)
XLA Modules:
  0.0 118.9 jit_solution(9252507689739783280)
XLA Ops:
  0.6 114.5 %exchange.1 = (f32[12288,384]{1,0:T(8,128)S(1)}, f32[1,384]{1,0:T(1,128)S(1)}, bf16[96,128]{1,0:T(8,128)(2,1)S(1)}) custom-call(bf16[384,12288]{1,0:T(8,128)(2,1)} %train.1, bf16[32,384]{1,0:T(8,128)(2,1)} %bitcast.4, bf16[32,12288]{1,0:T(8,128)(2,1)} %high.1, f32[1,96]{1,0:T(1,128)} %bitcast.5, f32[1,96]{1,0:T(1,128)} %bitcast.6), custom_call_target="tpu_custom_call" | custom-call | flops 300000000 | bytes 40000000 | tf_op jit(solution)/shard_map/exchange/pallas_call | solution.py:253
  115.1 3.8 %finish.1 = (bf16[12288,384]{1,0:T(8,128)(2,1)}, f32[384]{0:T(512)}, bf16[96,128]{1,0:T(8,128)(2,1)}) custom-call(f32[12288,384]{1,0:T(8,128)S(1)} %get-tuple-element.9.whole, f32[1,384]{1,0:T(1,128)S(1)} %get-tuple-element.10.scale, bf16[96,128]{1,0:T(8,128)(2,1)S(1)} %get-tuple-element.11.norm), custom_call_target="tpu_custom_call" | custom-call | flops 10000000 | bytes 10000000 | tf_op jit(solution)/shard_map/finish/pallas_call | solution.py:279

commit v6 on v5

--- a/solution.py
+++ b/solution.py
@@ -81,11 +81,6 @@
     ]
     for copy in get_norm:
         copy.start()
-    norm_all[core, y, slot] = jnp.zeros((1, 128), jnp.float32)
-    sums[...] = jnp.zeros_like(sums)
-    for copy in get_norm:
-        copy.wait()
-    norm_all[core, y, slot, :, pl.ds(0, PIECE)] = norm_mine[0] + norm_mine[1]
 
     def big(place, i, target):
         column = (place[0] * 8 + place[1] * 2 + target) * COLS
@@ -121,6 +116,11 @@
         copy.start()
     for dz, dx, dc in NEAR:
         pl.semaphore_signal(heard, inc=1, device_id=at(dz, dx, dc), device_id_type=MESH)
+    norm_all[core, y, slot] = jnp.zeros((1, 128), jnp.float32)
+    sums[...] = jnp.zeros_like(sums)
+    for copy in get_norm:
+        copy.wait()
+    norm_all[core, y, slot, :, pl.ds(0, PIECE)] = norm_mine[0] + norm_mine[1]
     get_low.wait()
     pl.semaphore_wait(heard, len(NEAR))
     stages = (

time: 119 us -> 119 us (level)
  no operation moved by 1% of the time
where the time goes in v6:
time: 119 us
  Pallas kernels  118 us (99%)
    pallas_call x1, Pallas kernels, local(): pl.pallas_call(exchange, name='exchange', out_shape=(pltpu.VMEM((D_MODEL,...  115 us
    pallas_call x1, Pallas kernels, local(): pl.pallas_call(finish, name='finish', out_shape=(jax.ShapeDtypeStruct((D_...  3.77 us

profile of v6, /device:TPU:1, one launch (start us, length us, event | category | flops | bytes accessed | tf_op | source)
XLA Modules:
  0.0 118.9 jit_solution(16197706926053032030)
XLA Ops:
  0.6 114.5 %exchange.1 = (f32[12288,384]{1,0:T(8,128)S(1)}, f32[1,384]{1,0:T(1,128)S(1)}, bf16[96,128]{1,0:T(8,128)(2,1)S(1)}) custom-call(bf16[384,12288]{1,0:T(8,128)(2,1)} %train.1, bf16[32,384]{1,0:T(8,128)(2,1)} %bitcast.4, bf16[32,12288]{1,0:T(8,128)(2,1)} %high.1, f32[1,96]{1,0:T(1,128)} %bitcast.5, f32[1,96]{1,0:T(1,128)} %bitcast.6), custom_call_target="tpu_custom_call" | custom-call | flops 300000000 | bytes 40000000 | tf_op jit(solution)/shard_map/exchange/pallas_call | solution.py:253
  115.1 3.8 %finish.1 = (bf16[12288,384]{1,0:T(8,128)(2,1)}, f32[384]{0:T(512)}, bf16[96,128]{1,0:T(8,128)(2,1)}) custom-call(f32[12288,384]{1,0:T(8,128)S(1)} %get-tuple-element.9.whole, f32[1,384]{1,0:T(1,128)S(1)} %get-tuple-element.10.scale, bf16[96,128]{1,0:T(8,128)(2,1)S(1)} %get-tuple-element.11.norm), custom_call_target="tpu_custom_call" | custom-call | flops 10000000 | bytes 10000000 | tf_op jit(solution)/shard_map/finish/pallas_call | solution.py:279
